TPU v7x, 32 devices: a whole 2x2x4 slice. The times are simulated.
32 devices in a mesh: dp: 4 (over x, core), half: 2 (over y), own: 4 (over z).
Axes of the slice: x: 2, y: 2, z: 4, core: 2. Of those that a mesh axis runs over, the one named last changes fastest.
Arguments:
- grad_parts: bfloat16 [4, 6, 1024, 1024], P('dp', None, ('half', 'own')), may hold values from -6 to 6
- owner_table: int32 [6, 1], replicated, may hold values from 0 to 3; in each aligned block of 6 rows (0 to 5, 6 to 11, ...) at most 2 rows name the same one
- left_basis: bfloat16 [8, 1024, 1024], P(('half', 'own')), may hold values from -0.1875 to 0.1875
- right_basis: bfloat16 [8, 1024, 1024], P(('half', 'own')), may hold values from -0.1875 to 0.1875
- first_moment: bfloat16 [8, 1024, 1024], P(('half', 'own'), 'dp'), may hold values from -6 to 6
- second_moment: bfloat16 [8, 1024, 1024], P(('half', 'own'), 'dp'), may hold values from 0.5 to 8
Outputs:
- update: bfloat16 [6, 1024, 1024], P(None, ('half', 'own'), 'dp')
Inputs may be any that keep to these rules, and one draw needn't show every extreme that they name: `owner_table`: every owner index is named by at least one block and by at most 2 blocks; some owner is named by exactly 2 blocks.
All inputs are finite; a program needn't handle non-finite values.
Results may differ from a plain program's by a relative error of at most 0.013.
Values may be sent and summed in bfloat16 or wider, within the bound.
A program may use at most 128 MiB of HBM per device.

v0:
```python
import jax
import jax.numpy as jnp
from jax import lax
from jax.sharding import PartitionSpec as P

beta_first = 0.9
beta_second = 0.95
bias_first = 1.0 - 0.9**10
bias_second = 1.0 - 0.95**10
epsilon = 1e-08


def slot_select(owner_table, owner_count, slot_count):
    owner_ids = owner_table[:, 0]
    positions = jnp.arange(owner_ids.shape[0], dtype=jnp.int32)
    shared = (owner_ids[:, None] == owner_ids[None, :]) & (positions[None, :] < positions[:, None])
    ranking = jnp.sum(shared.astype(jnp.int32), axis=1)
    slot_ids = ranking * owner_count + owner_ids
    slot_range = jnp.arange(slot_count, dtype=jnp.int32)
    return (slot_range[:, None] == slot_ids[None, :]).astype(jnp.bfloat16)


def local(grad_parts, owner_table, left_basis, right_basis, first_moment, second_moment):
    halves = lax.axis_size("half")
    owners = lax.axis_size("own")
    replicas = lax.axis_size("dp")
    block_count = grad_parts.shape[1]
    piece_rows = grad_parts.shape[2]
    block_width = grad_parts.shape[3]
    quarter = block_width // replicas
    offset = lax.axis_index("dp") * quarter
    summed = lax.psum_scatter(
        grad_parts[0].astype(jnp.float32).astype(jnp.bfloat16),
        "dp",
        scatter_dimension=2,
        tiled=True,
    )
    selector = slot_select(owner_table, owners, halves * owners)
    flat_grad = summed.reshape(block_count, piece_rows * quarter)
    packed = jnp.dot(selector, flat_grad, preferred_element_type=jnp.float32).astype(jnp.bfloat16)
    packed = packed.reshape(halves, owners, piece_rows, quarter)
    arrived = lax.all_to_all(
        lax.all_to_all(packed, "half", split_axis=0, concat_axis=0, tiled=True),
        "own",
        split_axis=1,
        concat_axis=1,
        tiled=True,
    )
    grad_block = arrived.reshape(block_width, quarter)
    left_matrix = left_basis[0]
    right_matrix = right_basis[0]
    right_rows = lax.dynamic_slice_in_dim(right_matrix, offset, quarter, 0)
    left_slice = lax.dynamic_slice_in_dim(left_matrix, offset, quarter, 1)
    projected = lax.dot_general(
        left_slice,
        lax.all_gather(grad_block, "dp", axis=1, tiled=True),
        (((0,), (0,)), ((), ())),
        preferred_element_type=jnp.float32,
    )
    rotated = jnp.dot(
        projected.astype(jnp.bfloat16), right_matrix, preferred_element_type=jnp.float32
    )
    first_new = beta_first * first_moment[0].astype(jnp.float32) + (1.0 - beta_first) * rotated
    second_new = (
        beta_second * second_moment[0].astype(jnp.float32) + (1.0 - beta_second) * rotated * rotated
    )
    direction = (first_new / bias_first / (jnp.sqrt(second_new / bias_second) + epsilon)).astype(
        jnp.bfloat16
    )
    partial_cols = lax.dot_general(
        lax.all_gather(direction, "dp", axis=0, tiled=True),
        right_rows,
        (((1,), (1,)), ((), ())),
        preferred_element_type=jnp.float32,
    )
    update_block = jnp.dot(
        left_matrix, partial_cols.astype(jnp.bfloat16), preferred_element_type=jnp.float32
    )
    outgoing = update_block.astype(jnp.bfloat16).reshape(halves, owners, piece_rows, quarter)
    returned = lax.all_to_all(
        lax.all_to_all(outgoing, "half", split_axis=0, concat_axis=0, tiled=True),
        "own",
        split_axis=1,
        concat_axis=1,
        tiled=True,
    )
    flat_back = returned.reshape(halves * owners, piece_rows * quarter)
    placed = lax.dot_general(
        selector, flat_back, (((0,), (0,)), ((), ())), preferred_element_type=jnp.float32
    )
    return placed.astype(jnp.bfloat16).reshape(block_count, piece_rows, quarter)


def solution(mesh):
    return jax.shard_map(
        local,
        mesh=mesh,
        in_specs=(
            P("dp", None, ("half", "own"), None),
            P(),
            P(("half", "own"), None, None),
            P(("half", "own"), None, None),
            P(("half", "own"), "dp", None),
            P(("half", "own"), "dp", None),
        ),
        out_specs=P(None, ("half", "own"), "dp"),
        check_vma=False,
    )
```

profile of v0, /device:TPU:0, one launch (start us, length us, event | category | flops | bytes accessed | tf_op | source)
XLA Modules:
  0.0 161.1 jit_solution(16821739264425904918)
XLA Ops:
  6.5 0.7 reduce-scatter.2.cloned.1.call-update
  7.3 0.0 all-gather.3.cloned.1.call-start
  7.3 0.9 convert_reduce_fusion
  8.2 0.7 multiply_add_fusion
  8.9 31.8 %reduce-scatter.2.cloned.1.call-done = bf16[6,128,256]{2,1,0:T(8,128)(2,1)} async-done(((bf16[6,128,1024]{2,1,0:T(8,128)(2,1)}), bf16[6,128,256]{2,1,0:T(8,128)(2,1)}) %reduce-scatter.2.cloned.1.call-update) | async-done | bytes 393232 | tf_op jit(solution)/shard_map/reduce_scatter | solution.py:32
  40.7 1.2 copy.26
  41.9 0.3 convolution_convert_fusion.1
  42.2 0.1 copy.27
  42.3 10.5 %all_to_all.20 = bf16[2,4,128,256]{3,2,1,0:T(8,128)(2,1)S(1)} all-to-all(bf16[2,4,128,256]{3,2,1,0:T(8,128)(2,1)S(1)} %bitcast.60), channel_id=1, replica_groups=mesh['dp'=4,'half'=2,'own'=4] {'half'}, dimensions={0} | all-to-all | bytes 1048576 | tf_op jit(solution)/shard_map/all_to_all | solution.py:43
  52.8 17.9 %all_to_all.21 = bf16[2,4,128,256]{3,2,0,1:T(8,128)(2,1)S(1)} all-to-all(bf16[2,4,128,256]{3,2,0,1:T(8,128)(2,1)S(1)} %copy.20), channel_id=1, replica_groups=mesh['dp'=4,'half'=2,'own'=4] {'own'}, dimensions={1} | all-to-all | bytes 1048576 | tf_op jit(solution)/shard_map/all_to_all | solution.py:42
  70.7 0.8 copy.21
  71.6 0.0 all-gather.3.cloned.1.call-update
  71.6 0.0 all-gather.5.cloned.1.call-start
  71.6 20.2 %all-gather.3.cloned.1.call-done = bf16[1024,1024]{1,0:T(8,128)(2,1)} async-done(((bf16[1024,256]{1,0:T(8,128)(2,1)}), bf16[1024,1024]{1,0:T(8,128)(2,1)}) %all-gather.3.cloned.1.call-update) | async-done | bytes 2097168 | tf_op jit(solution)/shard_map/all_gather | solution.py:56
  91.8 5.0 %fusion.16 = bf16[256,1024]{1,0:T(8,128)(2,1)} fusion(bf16[1,256,1024]{2,1,0:T(8,128)(2,1)S(1)} %copy-done.1, bf16[1,256,1024]{2,1,0:T(8,128)(2,1)S(1)} %copy-done.2, bf16[1,1024,1024]{2,1,0:T(8,128)(2,1)} %param.9, bf16[1024,1024]{1,0:T(8,128)(2,1)} %all-gather.3.cloned.1.call-done, bf16[1,1024,1024]{2,1,0:T(8,128)(2,1)S(1)} %copy-done, s32[]{:T(128)S(6)} %select_n.4), kind=kOutput, calls=%fused_computation.18 | convolution fusion | flops 1077673984 | bytes 6291460 | tf_op jit(solution)/shard_map/dot_general | solution.py:60
  96.8 0.0 all-gather.5.cloned.1.call-update
  96.8 22.7 %all-gather.5.cloned.1.call-done = bf16[1024,1024]{1,0:T(8,128)(2,1)} async-done(((bf16[256,1024]{1,0:T(8,128)(2,1)}), bf16[1024,1024]{1,0:T(8,128)(2,1)}) %all-gather.5.cloned.1.call-update) | async-done | bytes 2097168 | tf_op jit(solution)/shard_map/all_gather | solution.py:71
  119.5 4.0 %fusion.7 = bf16[1024,256]{0,1:T(8,128)(2,1)S(1)} fusion(bf16[1,1024,1024]{2,1,0:T(8,128)(2,1)S(1)} %copy-done, bf16[1024,1024]{1,0:T(8,128)(2,1)} %all-gather.5.cloned.1.call-done, bf16[1,1024,1024]{2,1,0:T(8,128)(2,1)} %param.9, s32[]{:T(128)S(6)} %select_n.4), kind=kOutput, calls=%fused_computation.10 | convolution fusion | flops 1074266112 | bytes 5242884 | tf_op jit(solution)/shard_map/dot_general | solution.py:76
  123.5 0.2 copy.25
  123.7 11.1 %all_to_all.22 = bf16[2,4,128,256]{3,2,1,0:T(8,128)(2,1)S(1)} all-to-all(bf16[2,4,128,256]{3,2,1,0:T(8,128)(2,1)S(1)} %bitcast.61), channel_id=1, replica_groups=mesh['dp'=4,'half'=2,'own'=4] {'half'}, dimensions={0} | all-to-all | bytes 1048576 | tf_op jit(solution)/shard_map/all_to_all | solution.py:81
  134.8 18.3 %all_to_all.23 = bf16[2,4,128,256]{3,2,0,1:T(8,128)(2,1)S(1)} all-to-all(bf16[2,4,128,256]{3,2,0,1:T(8,128)(2,1)S(1)} %copy.23), channel_id=1, replica_groups=mesh['dp'=4,'half'=2,'own'=4] {'own'}, dimensions={1} | all-to-all | bytes 1048576 | tf_op jit(solution)/shard_map/all_to_all | solution.py:80
  153.1 0.3 copy.28
  153.4 0.4 convolution_convert_fusion
  153.8 0.8 copy.31
  (10 shorter events, 0.1 us)
Async XLA Ops:
  6.5 85.3 %copy-start = (bf16[1,1024,1024]{2,1,0:T(8,128)(2,1)S(1)}, bf16[1,1024,1024]{2,1,0:T(8,128)(2,1)}, u32[]{:S(2)}) copy-start(bf16[1,1024,1024]{2,1,0:T(8,128)(2,1)} %param.8) | copy-start | bytes 6291460
  6.5 34.1 %reduce-scatter.2.cloned.1.call-start = ((), (), s32[]{:S(2)}) async-start(), calls=%async_computation.5 | async-start | bytes 1966080 | tf_op jit(solution)/shard_map/reduce_scatter | solution.py:32
  7.3 84.6 %all-gather.3.cloned.1.call-start = ((), (), s32[]{:S(2)}) async-start(), calls=%async_computation.6 | async-start | bytes 2621440 | tf_op jit(solution)/shard_map/all_gather | solution.py:56
  52.8 39.0 %copy-start.1 = (bf16[1,256,1024]{2,1,0:T(8,128)(2,1)S(1)}, bf16[1,256,1024]{2,1,0:T(8,128)(2,1)}, u32[]{:S(2)}) copy-start(bf16[1,256,1024]{2,1,0:T(8,128)(2,1)} %param.11) | copy-start | bytes 1572868
  52.8 39.0 %copy-start.2 = (bf16[1,256,1024]{2,1,0:T(8,128)(2,1)S(1)}, bf16[1,256,1024]{2,1,0:T(8,128)(2,1)}, u32[]{:S(2)}) copy-start(bf16[1,256,1024]{2,1,0:T(8,128)(2,1)} %param.10) | copy-start | bytes 1572868
  71.6 47.9 %all-gather.5.cloned.1.call-start = ((), (), s32[]{:S(2)}) async-start(), calls=%async_computation.7 | async-start | bytes 2621440 | tf_op jit(solution)/shard_map/all_gather | solution.py:71
Sparse Core Ops, SparseCore 0:
  9.9 30.7 reduce-scatter.1
  71.7 20.0 all-gather.2
  96.9 22.5 all-gather.4
where the time goes:
time: 162 us; the launch traced here: 161 us
  waiting for transfers between devices  75.4 us (47%)
  blocking collectives  57.7 us (36%)
  between operations  13.2 us (8%)
  matrix products  9.55 us (6%)
  local copies, waits for them, and re-layouts  3.59 us (2%)
    reduce_scatter x1, waiting for transfers between devices, local(): lax.psum_scatter(grad_parts[0].astype(jnp.float32).astype(jnp.bfloat16),...  31.8 us
    all_gather x1, waiting for transfers between devices, local(): lax.all_gather(direction, 'dp', axis=0, tiled=True)  22.7 us
    all_gather x1, waiting for transfers between devices, local(): lax.all_gather(grad_block, 'dp', axis=1, tiled=True)  20.2 us
    all_to_all x1, blocking collectives, local(): lax.all_to_all(lax.all_to_all(outgoing, 'half', split_axis=0, concat_axis...  18.3 us
    all_to_all x1, blocking collectives, local(): lax.all_to_all(lax.all_to_all(packed, 'half', split_axis=0, concat_axis=0...  17.9 us
    all_to_all x1, blocking collectives, local(): lax.all_to_all(outgoing, 'half', split_axis=0, concat_axis=0, tiled=True)  11.1 us
    all_to_all x1, blocking collectives, local(): lax.all_to_all(packed, 'half', split_axis=0, concat_axis=0, tiled=True)  10.5 us
    dot_general x1, matrix products, local(): jnp.dot(projected.astype(jnp.bfloat16), right_matrix, preferred_element_t...  4.95 us
  transfers between devices with their start and end apart: 3, of which 3 were waited for; matrix products, arithmetic and copies ran while one was open for 1% of the time, Pallas kernels for 0%

commit v1 on v0

--- a/solution.py
+++ b/solution.py
@@ -1,3 +1,4 @@
+import functools
 import jax
 import jax.numpy as jnp
 from jax import lax
@@ -8,6 +9,26 @@
 bias_first = 1.0 - 0.9**10
 bias_second = 1.0 - 0.95**10
 epsilon = 1e-08
+
+
+def assign_the_scales(state, axis_key):
+    nd = lax.axis_size(axis_key)
+    views = [(dd, (dd + 1) % nd) for dd in range(nd)]
+    nodes = [(dd, (dd - 1) % nd) for dd in range(nd)]
+    extra, upper = ([state], [state])
+    for _ in range(nd // 2):
+        arr_now = lax.ppermute(extra[-1], axis_name=axis_key, perm=views)
+        extra.append(arr_now)
+    for _ in [*range((nd - 1) // 2)]:
+        front = lax.ppermute(upper[-1], axis_key, nodes)
+        upper.append(front)
+    response = jnp.concatenate([*extra[::-1], *upper[1:]], axis=0)
+    seen_now = lax.axis_index(axis_key)
+    k_now = jnp.roll(response, (seen_now - nd // 2) * state.shape[0], axis=0)
+    return k_now
+
+
+return_all_lane = functools.partial(assign_the_scales, axis_key="dp")
 
 
 def slot_select(owner_table, owner_count, slot_count):
@@ -68,7 +89,7 @@
         jnp.bfloat16
     )
     partial_cols = lax.dot_general(
-        lax.all_gather(direction, "dp", axis=0, tiled=True),
+        return_all_lane(direction),
         right_rows,
         (((1,), (1,)), ((), ())),
         preferred_element_type=jnp.float32,

time: 162 us -> 167 us (1.031)
  local copies, waits for them, and re-layouts: 3.59 us -> 14.4 us
  blocking collectives: 57.7 us -> 52.1 us
  waiting for transfers between devices: 75.4 us -> 73 us
  starting transfers between devices: 0.08 us -> 2.09 us
    all_gather x1 -> x0, waiting for transfers between devices: 22.7 us -> none  [local(): lax.all_gather(direction, 'dp', axis=0, tiled=True)]
    ppermute x0 -> x3, waiting for transfers between devices: none -> 20.3 us  [the longest x2 20.3 us: assign_the_scales(): arr_now = lax.ppermute(extra[-1], axis_name=axis_key, perm=views)]
    unnamed x10 -> x15, local copies, waits for them, and re-layouts: 2.45 us -> 11.4 us
    all_to_all x1, blocking collectives: 18.3 us -> 14.9 us  [local(): lax.all_to_all(lax.all_to_all(outgoing, 'half', split_axis=0, concat_axis...]
    all_to_all x1, blocking collectives: 11.1 us -> 8.99 us  [local(): lax.all_to_all(outgoing, 'half', split_axis=0, concat_axis=0, tiled=True)]
    ppermute x0 -> x3, starting transfers between devices: none -> 2.05 us  [the longest x1 1.74 us: assign_the_scales(): front = lax.ppermute(upper[-1], axis_key, nodes)]
    concatenate x0 -> x1, local copies, waits for them, and re-layouts: none -> 1.87 us  [assign_the_scales(): k_now = jnp.roll(response, (seen_now - nd // 2) * state.shape[0], axis=0)]
  transfers between devices with their start and end apart: 3 -> 5, of which waited for: 3 -> 4; matrix products, arithmetic and copies ran while one was open for 1% -> 3% of each run, Pallas kernels for 0% -> 0%
where the time goes in v1:
time: 167 us; the launch traced here: 165 us
  waiting for transfers between devices  73 us (44%)
  blocking collectives  52.1 us (31%)
  local copies, waits for them, and re-layouts  14.4 us (9%)
  between operations  13.5 us (8%)
  matrix products  8.83 us (5%)
  starting transfers between devices  2.09 us (1%)
    reduce_scatter x1, waiting for transfers between devices, local(): lax.psum_scatter(grad_parts[0].astype(jnp.float32).astype(jnp.bfloat16),...  31.8 us
    ppermute x2, waiting for transfers between devices, assign_the_scales(): arr_now = lax.ppermute(extra[-1], axis_name=axis_key, perm=views)  20.3 us
    all_gather x1, waiting for transfers between devices, local(): lax.all_gather(grad_block, 'dp', axis=1, tiled=True)  20.2 us
    all_to_all x1, blocking collectives, local(): lax.all_to_all(lax.all_to_all(packed, 'half', split_axis=0, concat_axis=0...  17.7 us
    all_to_all x1, blocking collectives, local(): lax.all_to_all(lax.all_to_all(outgoing, 'half', split_axis=0, concat_axis...  14.9 us
    unnamed x15, local copies, waits for them, and re-layouts  11.4 us
    all_to_all x1, blocking collectives, local(): lax.all_to_all(packed, 'half', split_axis=0, concat_axis=0, tiled=True)  10.5 us
    all_to_all x1, blocking collectives, local(): lax.all_to_all(outgoing, 'half', split_axis=0, concat_axis=0, tiled=True)  8.99 us
  transfers between devices with their start and end apart: 5, of which 4 were waited for; matrix products, arithmetic and copies ran while one was open for 3% of the time, Pallas kernels for 0%

profile of v1, /device:TPU:0, one launch (start us, length us, event | category | flops | bytes accessed | tf_op | source)
XLA Modules:
  0.0 165.5 jit_solution(10139168291565246528)
XLA Ops:
  6.5 0.7 reduce-scatter.2.cloned.1.call-update
  7.3 0.9 convert_reduce_fusion
  8.9 31.8 %reduce-scatter.2.cloned.1.call-done = bf16[6,128,256]{2,1,0:T(8,128)(2,1)} async-done(((bf16[6,128,1024]{2,1,0:T(8,128)(2,1)}), bf16[6,128,256]{2,1,0:T(8,128)(2,1)}) %reduce-scatter.2.cloned.1.call-update) | async-done | bytes 393232 | tf_op jit(solution)/shard_map/reduce_scatter | solution.py:53
  40.7 1.2 copy.26
  42.3 10.5 %all_to_all.20 = bf16[2,4,128,256]{3,2,1,0:T(8,128)(2,1)S(1)} all-to-all(bf16[2,4,128,256]{3,2,1,0:T(8,128)(2,1)S(1)} %bitcast.59), channel_id=1, replica_groups=mesh['dp'=4,'half'=2,'own'=4] {'half'}, dimensions={0} | all-to-all | bytes 1048576 | tf_op jit(solution)/shard_map/all_to_all | solution.py:64
  52.8 17.7 %all_to_all.21 = bf16[2,4,128,256]{3,2,0,1:T(8,128)(2,1)S(1)} all-to-all(bf16[2,4,128,256]{3,2,0,1:T(8,128)(2,1)S(1)} %copy.20), channel_id=1, replica_groups=mesh['dp'=4,'half'=2,'own'=4] {'own'}, dimensions={1} | all-to-all | bytes 1048576 | tf_op jit(solution)/shard_map/all_to_all | solution.py:63
  70.6 0.8 copy.21
  71.4 20.2 %all-gather.2.cloned.1.call-done = bf16[1024,1024]{1,0:T(8,128)(2,1)} async-done(((bf16[1024,256]{1,0:T(8,128)(2,1)}), bf16[1024,1024]{1,0:T(8,128)(2,1)}) %all-gather.2.cloned.1.call-update) | async-done | bytes 2097168 | tf_op jit(solution)/shard_map/all_gather | solution.py:77
  91.7 4.2 %fusion.21 = bf16[256,1024]{1,0:T(8,128)(2,1)S(1)} fusion(bf16[1,256,1024]{2,1,0:T(8,128)(2,1)S(1)} %copy-done.1, bf16[1,256,1024]{2,1,0:T(8,128)(2,1)} %param.10, bf16[1,1024,1024]{2,1,0:T(8,128)(2,1)} %param.9, bf16[1024,1024]{1,0:T(8,128)(2,1)} %all-gather.2.cloned.1.call-done, bf16[1,1024,1024]{2,1,0:T(8,128)(2,1)S(1)} %copy-done, s32[]{:T(128)S(6)} %select_n.17), kind=kOutput, calls=%fused_computation.20 | convolution fusion | flops 1077673984 | bytes 6291460 | tf_op jit(solution)/shard_map/dot_general | solution.py:81
  96.2 8.3 %collective-permute-done = bf16[256,1024]{1,0:T(8,128)(2,1)S(1)} collective-permute-done((bf16[256,1024]{1,0:T(8,128)(2,1)S(1)}, bf16[256,1024]{1,0:T(8,128)(2,1)S(1)}, u32[]{:S(2)}, u32[]{:S(2)}) %collective-permute-start) | collective-permute-done | bytes 524320 | tf_op jit(solution)/shard_map/ppermute | solution.py:20
  104.6 1.7 %collective-permute-start.2 = (bf16[256,1024]{1,0:T(8,128)(2,1)S(1)}, bf16[256,1024]{1,0:T(8,128)(2,1)}, u32[]{:S(2)}, u32[]{:S(2)}) collective-permute-start(bf16[256,1024]{1,0:T(8,128)(2,1)S(1)} %fusion.21), channel_id=1, source_target_pairs={{0,24},{8,0},{16,8},{24,16},{1,25},{9,1},{17,9},{25,17},{2,26},{10... | collective-permute-start | bytes 1572872 | tf_op jit(solution)/shard_map/ppermute | solution.py:23
  106.3 11.9 %collective-permute-done.1 = bf16[256,1024]{1,0:T(8,128)(2,1)} collective-permute-done((bf16[256,1024]{1,0:T(8,128)(2,1)S(1)}, bf16[256,1024]{1,0:T(8,128)(2,1)}, u32[]{:S(2)}, u32[]{:S(2)}) %collective-permute-start.1) | collective-permute-done | bytes 524320 | tf_op jit(solution)/shard_map/ppermute | solution.py:20
  118.3 1.9 %constant_dynamic-update-slice_fusion.7 = bf16[2048,1024]{1,0:T(8,128)(2,1)} fusion(bf16[256,1024]{1,0:T(8,128)(2,1)} %collective-permute-done.1), kind=kLoop, calls=%fused_computation.33 | loop fusion | bytes 1048576
  120.1 0.8 constant_dynamic-update-slice_fusion.6
  120.9 0.8 constant_dynamic-update-slice_fusion.5
  121.8 1.9 %constant_dynamic-update-slice_fusion.4 = bf16[2048,1024]{1,0:T(8,128)(2,1)} fusion(bf16[2048,1024]{1,0:T(8,128)(2,1)} %constant_dynamic-update-slice_fusion.5, bf16[256,1024]{1,0:T(8,128)(2,1)} %collective-permute-done.2), kind=kLoop, calls=%fused_computation.30 | loop fusion | bytes 1048576
  123.6 1.9 %constant_dynamic-update-slice_fusion.3 = bf16[2048,1024]{1,0:T(8,128)(2,1)} fusion(bf16[2048,1024]{1,0:T(8,128)(2,1)} %constant_dynamic-update-slice_fusion.4, bf16[256,1024]{1,0:T(8,128)(2,1)} %collective-permute-done.1), kind=kLoop, calls=%fused_computation.29 | loop fusion | bytes 1048576
  125.5 0.8 constant_dynamic-update-slice_fusion.2
  126.3 0.8 constant_dynamic-update-slice_fusion.1
  127.2 1.9 %constant_dynamic-update-slice_fusion = bf16[2048,1024]{1,0:T(8,128)(2,1)} fusion(bf16[2048,1024]{1,0:T(8,128)(2,1)} %constant_dynamic-update-slice_fusion.1, bf16[256,1024]{1,0:T(8,128)(2,1)} %collective-permute-done.2), kind=kLoop, calls=%fused_computation.26 | loop fusion | bytes 1048576 | tf_op jit(solution)/shard_map/jit(_roll_dynamic)/concatenate | solution.py:27
  129.1 4.0 %fusion.12 = bf16[1024,256]{0,1:T(8,128)(2,1)S(1)} fusion(bf16[1,1024,1024]{2,1,0:T(8,128)(2,1)S(1)} %copy-done, bf16[2048,1024]{1,0:T(8,128)(2,1)} %constant_dynamic-update-slice_fusion, s32[]{:T(128)S(6)} %select_n.19, bf16[1,1024,1024]{2,1,0:T(8,128)(2,1)} %param.9, s32[]{:T(128)S(6)} %select_n.17), kind=kOutput, calls=%fused_computation.12 | convolution fusion | flops 1074266112 | bytes 5242888 | tf_op jit(solution)/shard_map/dot_general | solution.py:97
  133.2 9.0 %all_to_all.22 = bf16[2,4,128,256]{3,2,1,0:T(8,128)(2,1)S(1)} all-to-all(bf16[2,4,128,256]{3,2,1,0:T(8,128)(2,1)S(1)} %bitcast.60), channel_id=1, replica_groups=mesh['dp'=4,'half'=2,'own'=4] {'half'}, dimensions={0} | all-to-all | bytes 1048576 | tf_op jit(solution)/shard_map/all_to_all | solution.py:102
  142.3 14.9 %all_to_all.23 = bf16[2,4,128,256]{3,2,0,1:T(8,128)(2,1)S(1)} all-to-all(bf16[2,4,128,256]{3,2,0,1:T(8,128)(2,1)S(1)} %copy.23), channel_id=1, replica_groups=mesh['dp'=4,'half'=2,'own'=4] {'own'}, dimensions={1} | all-to-all | bytes 1048576 | tf_op jit(solution)/shard_map/all_to_all | solution.py:101
  157.8 0.8 copy.31
  (19 shorter events, 2.4 us)
Async XLA Ops:
  6.5 85.1 %copy-start = (bf16[1,1024,1024]{2,1,0:T(8,128)(2,1)S(1)}, bf16[1,1024,1024]{2,1,0:T(8,128)(2,1)}, u32[]{:S(2)}) copy-start(bf16[1,1024,1024]{2,1,0:T(8,128)(2,1)} %param.8) | copy-start | bytes 6291460
  6.5 34.1 %reduce-scatter.2.cloned.1.call-start = ((), (), s32[]{:S(2)}) async-start(), calls=%async_computation.5 | async-start | bytes 1966080 | tf_op jit(solution)/shard_map/reduce_scatter | solution.py:53
  7.3 84.4 %copy-start.1 = (bf16[1,256,1024]{2,1,0:T(8,128)(2,1)S(1)}, bf16[1,256,1024]{2,1,0:T(8,128)(2,1)}, u32[]{:S(2)}) copy-start(bf16[1,256,1024]{2,1,0:T(8,128)(2,1)} %param.11) | copy-start | bytes 1572868
  7.3 84.4 %all-gather.2.cloned.1.call-start = ((), (), s32[]{:S(2)}) async-start(), calls=%async_computation.6 | async-start | bytes 2621440 | tf_op jit(solution)/shard_map/all_gather | solution.py:77
  95.9 8.7 %collective-permute-start = (bf16[256,1024]{1,0:T(8,128)(2,1)S(1)}, bf16[256,1024]{1,0:T(8,128)(2,1)S(1)}, u32[]{:S(2)}, u32[]{:S(2)}) collective-permute-start(bf16[256,1024]{1,0:T(8,128)(2,1)S(1)} %fusion.21), channel_id=1, source_target_pairs={{0,8},{8,16},{16,24},{24,0},{1,9},{9,17},{17,25},{25,1},{2,10},{10... | collective-permute-start | bytes 1572872 | tf_op jit(solution)/shard_map/ppermute | solution.py:20
  104.6 13.7 %collective-permute-start.1 = (bf16[256,1024]{1,0:T(8,128)(2,1)S(1)}, bf16[256,1024]{1,0:T(8,128)(2,1)}, u32[]{:S(2)}, u32[]{:S(2)}) collective-permute-start(bf16[256,1024]{1,0:T(8,128)(2,1)S(1)} %collective-permute-done), channel_id=1, source_target_pairs={{0,8},{8,16},{16,24},{24,0},{1,9},{9,17},{17,25},{25,1},{2,10},{10... | collective-permute-start | bytes 1572872 | tf_op jit(solution)/shard_map/ppermute | solution.py:20
  104.6 17.2 %collective-permute-start.2 = (bf16[256,1024]{1,0:T(8,128)(2,1)S(1)}, bf16[256,1024]{1,0:T(8,128)(2,1)}, u32[]{:S(2)}, u32[]{:S(2)}) collective-permute-start(bf16[256,1024]{1,0:T(8,128)(2,1)S(1)} %fusion.21), channel_id=1, source_target_pairs={{0,24},{8,0},{16,8},{24,16},{1,25},{9,1},{17,9},{25,17},{2,26},{10... | collective-permute-start | bytes 1572872 | tf_op jit(solution)/shard_map/ppermute | solution.py:23
Sparse Core Ops, SparseCore 0:
  9.9 30.7 reduce-scatter.1
  71.6 20.0 all-gather.1
